TPU v7x, 256 devices: a 2x2x32 block of a 4x8x32 slice. The times are simulated.
256 devices in a mesh: grp: 4 (over y, x), wide: 64 (over z, core).
Axes of the slice: x: 2, y: 2, z: 32, core: 2. Of those that a mesh axis runs over, the one named last changes fastest.
The devices are a block of a 4x8x32 slice.
Arguments:
- kv_prefill: bfloat16 [2, 32, 8, 8192, 128], P(None, 'grp', None, 'wide'), parts along dimension 1, may hold values from -4 to 4
- queries: bfloat16 [256, 1024], P(('grp', 'wide')), parts along dimension 0, may hold values from -512 to 512
- fresh_kv: bfloat16 [2, 256, 128], P(None, ('grp', 'wide')), parts along dimension 1, may hold values from -4 to 4
- lengths: int32 [32], P('grp'), parts along dimension 0, may hold values from 1 to 8191, as said below
- decode_slot_pair: int32 [256], P('grp'), parts along dimension 0, may hold values from 0 to 63, each once
Outputs:
- decode_cache: bfloat16 [2, 256, 8192, 128], P(None, ('grp', 'wide')), parts along dimension 1
- attention: bfloat16 [256, 1024], P(('grp', 'wide')), parts along dimension 0
There are 4 independent parts, one for each index of `grp`. A program takes and returns all parts, laid end to end along the dimension named above; each array names one. Nothing has to cross between parts.
Inputs may be any that keep to these rules, and one draw needn't show every extreme that they name: `lengths`: every draw holds a sequence of length 8191 and one of length 1. `decode_slot_pair`: slot j lies on the device of wide with index j // (64 / 64).
All inputs are finite; a program needn't handle non-finite values.
Results may differ from a plain program's by a relative error of at most 0.001.
Values may be sent and summed in bfloat16 or wider, within the bound.
A program may use at most 64 MiB of HBM per device.

v0:
```python
import math

import jax
import jax.numpy as jnp
from jax import lax
from jax.sharding import PartitionSpec as P

NEG_FILL = -1e30


def laid_out(tiles, dim):
    lengths = list(tiles.shape[1:])
    lengths[dim] *= tiles.shape[0]
    return jnp.moveaxis(tiles, 0, dim).reshape(lengths)


def one_gather(arrays, axis, dims):
    flat = jnp.concatenate([a.reshape(-1) for a in arrays])
    lines, at, finished = (lax.all_gather(flat, axis), 0, [])
    for a, dim in zip(arrays, dims):
        tiles = lines[:, at : at + a.size].reshape(-1, *a.shape)
        finished.append(laid_out(tiles, dim))
        at += a.size
    return tuple(finished)


def local(kv_prefill, queries, fresh_kv, lengths, decode_slot_pair):
    devices = lax.axis_size("wide")
    my_rank = lax.axis_index("wide")
    seq_count = kv_prefill.shape[1]
    head_count = kv_prefill.shape[2]
    local_len = kv_prefill.shape[3]
    head_dim = kv_prefill.shape[4]
    item_count = seq_count * head_count
    per_device = item_count // devices
    group_size = queries.shape[1] // head_dim
    softmax_scale = 1.0 / math.sqrt(head_dim)
    pair_length = jnp.repeat(lengths, head_count)
    local_pos = my_rank * local_len + jnp.arange(local_len, dtype=jnp.int32)
    kv_rows = kv_prefill.reshape(2, item_count, local_len, head_dim)
    in_prompt = local_pos[None, :] < pair_length[:, None]
    kv_rows = jnp.where(in_prompt[None, :, :, None], kv_rows, jnp.zeros((), kv_rows.dtype))
    ordered = jnp.take(kv_rows, decode_slot_pair, axis=1)
    gathered_q, gathered_new = one_gather((queries, fresh_kv), "wide", (0, 1))
    own_slots = lax.dynamic_slice_in_dim(decode_slot_pair, my_rank * per_device, per_device)
    own_len = jnp.take(pair_length, own_slots)
    own_q = jnp.take(gathered_q, own_slots, axis=0).reshape(per_device, group_size, head_dim)
    own_new = jnp.take(gathered_new, own_slots, axis=1)
    decode_cache = lax.all_to_all(ordered, "wide", split_axis=1, concat_axis=2, tiled=True)
    full_len = decode_cache.shape[2]
    full_pos = jnp.arange(full_len, dtype=jnp.int32)
    at_new = full_pos[None, :] == own_len[:, None]
    decode_cache = jnp.where(at_new[None, :, :, None], own_new[:, :, None, :], decode_cache)
    tile_length = min(512, full_len)
    tile_count = (jnp.max(own_len) + tile_length) // tile_length

    def attend_tile(tile_index, carry):
        run_max, run_sum, run_out = carry
        start = tile_index * tile_length
        key_tile = lax.dynamic_slice_in_dim(decode_cache[0], start, tile_length, 1)
        value_tile = lax.dynamic_slice_in_dim(decode_cache[1], start, tile_length, 1)
        scores = (
            jnp.einsum("igd,ibd->igb", own_q, key_tile, preferred_element_type=jnp.float32)
            * softmax_scale
        )
        tile_pos = start + jnp.arange(tile_length, dtype=jnp.int32)
        visible = tile_pos[None, :] <= own_len[:, None]
        scores = jnp.where(visible[:, None, :], scores, NEG_FILL)
        new_max = jnp.maximum(run_max, jnp.max(scores, axis=2))
        weights = jnp.where(visible[:, None, :], jnp.exp(scores - new_max[:, :, None]), 0.0)
        factor = jnp.exp(run_max - new_max)
        run_sum = run_sum * factor + jnp.sum(weights, axis=2)
        run_out = run_out * factor[:, :, None] + jnp.einsum(
            "igb,ibd->igd", weights, value_tile.astype(jnp.float32), precision=lax.Precision.HIGHEST
        )
        return (new_max, run_sum, run_out)

    start_carry = (
        jnp.full((per_device, group_size), NEG_FILL, jnp.float32),
        jnp.zeros((per_device, group_size), jnp.float32),
        jnp.zeros((per_device, group_size, head_dim), jnp.float32),
    )
    run_max, run_sum, run_out = lax.fori_loop(0, tile_count, attend_tile, start_carry)
    attention = run_out / run_sum[:, :, None]
    attention = attention.reshape(per_device, group_size * head_dim).astype(jnp.bfloat16)
    return (decode_cache, attention)


def solution(mesh):
    in_specs = (
        P(None, "grp", None, "wide", None),
        P(("grp", "wide"), None),
        P(None, ("grp", "wide"), None),
        P("grp"),
        P("grp"),
    )
    out_specs = (P(None, ("grp", "wide"), None, None), P(("grp", "wide"), None))
    return jax.shard_map(local, mesh=mesh, in_specs=in_specs, out_specs=out_specs, check_vma=False)
```

profile of v0, /device:TPU:45, one launch (start us, length us, event | category | flops | bytes accessed | tf_op | source)
XLA Modules:
  0.0 524.5 jit_solution(15470017661075900586)
XLA Ops:
  0.6 0.7 compare_and_fusion
  1.3 0.7 compare_select_fusion
  2.0 0.7 broadcast_in_dim.104
  2.9 5.2 %broadcast_select_fusion = bf16[2,64,128,128]{3,2,1,0:T(8,128)(2,1)} fusion(bf16[2,64,128,128]{3,2,1,0:T(8,128)(2,1)} %bitcast.66, pred[64,128]{1,0:T(8,128)(4,1)S(1)} %broadcast_compare_fusion), kind=kLoop, calls=%fused_computation.25 | loop fusion | flops 2097152 | bytes 8396800 | tf_op jit(solution)/shard_map/jit(_where)/select_n | solution.py:42
  8.1 5.2 gather_fusion
  13.3 4.6 select_bitcast_fusion
  17.9 33.7 %all-to-all-start = ((bf16[2,64,128,128]{3,2,0,1:T(8,128)(2,1)}), bf16[2,64,128,128]{3,2,0,1:T(8,128)(2,1)}, u32[]{:S(2)}, u32[]{:S(2)}) async-start(bf16[2,64,128,128]{3,2,0,1:T(8,128)(2,1)} %select_bitcast_fusion), calls=%async_computation | async-start | bytes 8388608 | tf_op jit(solution)/shard_map/all_to_all | solution.py:49
  51.6 0.6 dynamic_slice.9
  53.9 0.7 dynamic-slice.10
  55.4 411.5 %all-gather.1 = bf16[64,1,1280]{2,1,0:T(2,128)(2,1)S(1)} all-gather(bf16[1,1,1280]{2,1,0:T(2,128)(2,1)S(1)} %reshape.281), channel_id=2, replica_groups=mesh['grp'=4,'wide'=64] {'wide'}, dimensions={0}, use_global_device_ids=true | all-gather | bytes 166400 | tf_op jit(solution)/shard_map/all_gather | solution.py:19
  467.1 2.5 copy.14
  469.6 5.2 bitcast_select_fusion
  474.8 49.1 %while.17 = (s32[]{:T(128)}, f32[1,8]{1,0:T(1,128)S(1)}, f32[1,8]{1,0:T(1,128)S(1)}, f32[1,8,128]{2,1,0:T(8,128)S(1)}, s32[]{:T(128)}, /*index=5*/s32[1]{0:T(128...) while((s32[]{:T(128)}, f32[1,8]{1,0:T(1,128)S(1)}, ...), condition=%wide.region_3.4_spmd, body=%wide.region_0.0_spmd.sunk | while | flops 7375902 | bytes 8713843 | solution.py:83
  474.8 2.5 fusion.27
  477.3 0.3 fusion.28
  477.5 0.2 fusion.31
  477.8 0.2 fusion.30
  478.0 2.5 fusion.27
  480.5 0.3 fusion.28
  480.8 0.2 fusion.31
  481.1 0.2 fusion.30
  481.3 2.5 fusion.27
  483.8 0.3 fusion.28
  484.1 0.2 fusion.31
  484.3 0.2 fusion.30
  484.6 2.5 fusion.27
  487.1 0.3 fusion.28
  487.4 0.2 fusion.31
  487.6 0.2 fusion.30
  487.9 2.5 fusion.27
  490.4 0.3 fusion.28
  490.6 0.2 fusion.31
  490.9 0.2 fusion.30
  491.1 2.5 fusion.27
  493.6 0.3 fusion.28
  493.9 0.2 fusion.31
  494.4 2.5 fusion.27
  496.9 0.3 fusion.28
  497.2 0.2 fusion.31
  497.7 2.5 fusion.27
  500.2 0.3 fusion.28
  500.5 0.2 fusion.31
  501.0 2.5 fusion.27
  503.5 0.3 fusion.28
  503.7 0.2 fusion.31
  504.2 2.5 fusion.27
  506.7 0.3 fusion.28
  507.0 0.2 fusion.31
  507.5 2.5 fusion.27
  510.0 0.3 fusion.28
  510.3 0.2 fusion.31
  510.8 2.5 fusion.27
  513.3 0.3 fusion.28
  513.6 0.2 fusion.31
  514.0 2.5 fusion.27
  516.5 0.3 fusion.28
  516.8 0.2 fusion.31
  517.3 2.5 fusion.27
  519.8 0.3 fusion.28
  520.1 0.2 fusion.31
  520.6 2.5 fusion.27
  523.1 0.3 fusion.28
  523.4 0.2 fusion.31
  523.9 0.6 copy.22
  (95 shorter events, 2.8 us)
Async XLA Ops:
  17.9 33.7 %copy-start.2 = (s32[64]{0:T(128)S(1)}, s32[64]{0:T(128)}, u32[]{:S(2)}) copy-start(s32[64]{0:T(128)} %param.11) | copy-start | bytes 772
  17.9 37.3 %copy-start = (bf16[1,1024]{1,0:T(2,128)(2,1)S(1)}, bf16[1,1024]{1,0:T(2,128)(2,1)}, u32[]{:S(2)}) copy-start(bf16[1,1024]{1,0:T(2,128)(2,1)} %param.8) | copy-start | bytes 6148
  17.9 37.4 %copy-start.1 = (bf16[2,1,128]{2,0,1:T(2,128)(2,1)S(1)}, bf16[2,1,128]{2,0,1:T(2,128)(2,1)}, u32[]{:S(2)}) copy-start(bf16[2,1,128]{2,0,1:T(2,128)(2,1)} %param.9) | copy-start | bytes 1540
  17.9 449.1 %all-to-all-start = ((bf16[2,64,128,128]{3,2,0,1:T(8,128)(2,1)}), bf16[2,64,128,128]{3,2,0,1:T(8,128)(2,1)}, u32[]{:S(2)}, u32[]{:S(2)}) async-start(bf16[2,64,128,128]{3,2,0,1:T(8,128)(2,1)} %select_bitcast_fusion), calls=%async_computation | async-start | bytes 8388608 | tf_op jit(solution)/shard_map/all_to_all | solution.py:49
where the time goes:
time: 529 us; the launch traced here: 525 us
  blocking collectives  412 us (78%)
  local copies, waits for them, and re-layouts  47.9 us (9%)
  starting transfers between devices  33.7 us (6%)
  other arithmetic  19.9 us (4%)
  matrix products  7.5 us (1%)
    all_gather x1, blocking collectives, one_gather(): lines, at, finished = (lax.all_gather(flat, axis), 0, [])  412 us
    slice x15, local copies, waits for them, and re-layouts, attend_tile(): decode_cache[1]  37.5 us
    all_to_all x1, starting transfers between devices, local(): lax.all_to_all(ordered, 'wide', split_axis=1, concat_axis=2, tiled=True)  33.7 us
  transfers between devices with their start and end apart: 1, of which 0 were waited for; matrix products, arithmetic and copies ran while one was open for 0% of the time, Pallas kernels for 0%

commit v1 on v0

v1 whole, which is shorter than its diff:
```python
import functools
import math

import jax
import jax.numpy as jnp
from jax import lax
from jax.experimental import pallas as pl
from jax.experimental.pallas import tpu as pltpu
from jax.sharding import PartitionSpec as P

MESH = pl.DeviceIdType.MESH
NEG_FILL = -1e30
ROW_TILE = 16
CHUNK = 1024


def exchange_kernel(
    devices,
    perm_ref,
    query_ref,
    fresh_ref,
    kv_ref,
    gathered_ref,
    own_ref,
    stage,
    ordered,
    rows,
    stage_sem,
    local_sem,
    send_sem,
    recv_sem,
    row_send,
    row_recv,
    near_sem,
):
    chips = devices // 2
    half = chips // 2
    me = lax.axis_index("wide")
    chip = me // 2
    core = lax.rem(me, 2)
    partner = chip * 2 + 1 - core
    local_len = kv_ref.shape[2]

    def device(offset, which):
        return lax.rem(chip + offset + chips, chips) * 2 + which

    def remote(src, dst, send, recv, target):
        return pltpu.make_async_remote_copy(
            src_ref=src,
            dst_ref=dst,
            send_sem=send,
            recv_sem=recv,
            device_id={"wide": target},
            device_id_type=MESH,
        )

    def signal(sem, target):
        pl.semaphore_signal(sem, inc=1, device_id={"wide": target}, device_id_type=MESH)

    barrier = pltpu.get_barrier_semaphore()
    signal(barrier, partner)
    for offset in (1, -1):
        for which in (0, 1):
            signal(barrier, device(offset, which))
    fill = pltpu.make_async_copy(kv_ref, stage, stage_sem)
    fill.start()
    query = query_ref[...].astype(jnp.float32)
    head_dim = kv_ref.shape[3]
    group_size = query.shape[1] // head_dim
    parts = [query[:, g * head_dim : (g + 1) * head_dim] for g in range(group_size)]
    parts.append(fresh_ref[...].astype(jnp.float32))
    parts.append(jnp.zeros((ROW_TILE - group_size - 2, head_dim), jnp.float32))
    rows[0, 0] = jnp.concatenate(parts, axis=0).astype(jnp.bfloat16)
    fill.wait()

    def place(slot, carry):
        ordered[slot] = stage[:, perm_ref[slot]]
        return carry

    lax.fori_loop(0, devices, place, 0)
    pl.semaphore_wait(barrier, 5)

    final = gathered_ref.at[:, pl.ds(me * local_len, local_len)]
    keep = pltpu.make_async_copy(ordered.at[me], final, local_sem)
    keep.start()

    def send_block(target):
        remote(ordered.at[target], final, send_sem, recv_sem, target).start()

    def send_both(distance, cores=(0, 1)):
        for which in cores:
            for sign in (1, -1):
                send_block(device(sign * distance, which))

    def widen(level):
        reach = 1 << level
        for sign in (1, -1):
            signal(near_sem.at[level], device(sign * reach, core))
        pl.semaphore_wait(near_sem.at[level], 2)

    send_block(partner)
    send_both(1, (0,))
    sent_to = 1
    level = 0
    while (1 << level) < half:
        widen(level)
        level += 1
        if level < half.bit_length() - 1:
            for distance in range(sent_to + 1, min((1 << level), 5) + 1):
                send_both(distance)
                sent_to = distance

    turn = 1 - 2 * core

    def row_copy(step):
        size = 1 << step
        return remote(
            rows.at[0, pl.ds(0, size)],
            rows.at[0, pl.ds(size, size)],
            row_send.at[step],
            row_recv.at[step],
            device(turn * (chips >> (step + 1)), core),
        )

    send_block(device(half, 0))
    send_block(device(half, 1))
    row_steps = chips.bit_length() - 1
    row_copy(0).start()
    step = 0
    distances = list(range(half - 1, sent_to, -1))
    for number, distance in enumerate(distances):
        send_both(distance)
        if number % 2 == 1:
            if step < row_steps:
                row_copy(step).wait()
                step += 1
                if step < row_steps:
                    row_copy(step).start()
    send_both(1, (1,))
    while step < row_steps:
        row_copy(step).wait()
        step += 1
        if step < row_steps:
            row_copy(step).start()
    across = remote(rows.at[0], rows.at[1], row_send.at[row_steps], row_recv.at[row_steps], partner)
    across.start()
    across.wait()

    item = perm_ref[me]
    item_core = lax.rem(item, 2)
    same = 1 - lax.rem(item_core + core, 2)
    offset = lax.rem((1 - 2 * item_core) * (chip - item // 2) + chips, chips)
    place_of = 0
    for bit in range(row_steps):
        place_of += lax.rem(offset // (1 << bit), 2) * (chips >> (bit + 1))
    own_ref[...] = rows[1 - same, place_of]

    keep.wait()
    many = ordered.at[pl.ds(0, devices - 1)]
    everything = remote(many, many, send_sem, recv_sem, partner)
    everything.wait_send()
    everything.wait_recv()


def exchange(perm, queries, fresh, kv, devices):
    items, local_len, head_dim = kv.shape[1:]
    chips = devices // 2
    row_steps = chips.bit_length() - 1
    any_space = pl.BlockSpec(memory_space=pl.ANY)
    vmem = pl.BlockSpec(memory_space=pltpu.VMEM)
    block = (2, local_len, head_dim)
    return pl.pallas_call(
        functools.partial(exchange_kernel, devices),
        out_shape=(
            jax.ShapeDtypeStruct((2, devices * local_len, head_dim), kv.dtype),
            jax.ShapeDtypeStruct((ROW_TILE, head_dim), kv.dtype),
        ),
        in_specs=[pl.BlockSpec(memory_space=pltpu.SMEM), vmem, vmem, any_space],
        out_specs=(any_space, vmem),
        scratch_shapes=[
            pltpu.VMEM((2, items, local_len, head_dim), kv.dtype),
            pltpu.VMEM((items, *block), kv.dtype),
            pltpu.VMEM((2, chips, ROW_TILE, head_dim), kv.dtype),
            pltpu.SemaphoreType.DMA,
            pltpu.SemaphoreType.DMA,
            pltpu.SemaphoreType.DMA,
            pltpu.SemaphoreType.DMA,
            pltpu.SemaphoreType.DMA((row_steps + 1,)),
            pltpu.SemaphoreType.DMA((row_steps + 1,)),
            pltpu.SemaphoreType.REGULAR((row_steps,)),
        ],
        compiler_params=pltpu.CompilerParams(collective_id=0, has_side_effects=True),
        name="exchange",
    )(perm, queries, fresh, kv)


def attend_kernel(
    head_count, perm_ref, length_ref, own_ref, gathered_ref, cache_ref, out_ref,
    tiles, zeros, scores, in_sems, out_sem,
):
    me = lax.axis_index("wide")
    length = length_ref[perm_ref[me] // head_count]
    total_len, head_dim = tiles.shape[1:]
    group_size = scores.shape[0]
    chunk = zeros.shape[0]
    chunk_count = total_len // chunk
    live = length // chunk + 1
    last = live - 1

    def part(ref, kind, c):
        return ref.at[kind, pl.ds(pl.multiple_of(c * chunk, chunk), chunk)]

    def fetch(kind, c):
        return pltpu.make_async_copy(part(gathered_ref, kind, c), part(tiles, kind, c), in_sems.at[kind, c])

    def store(kind, c):
        return pltpu.make_async_copy(part(tiles, kind, c), part(cache_ref, kind, c), out_sem)

    def blank(kind, c):
        return pltpu.make_async_copy(zeros, part(cache_ref, kind, c), out_sem)

    for kind in (0, 1):
        lax.fori_loop(0, live, lambda c, x, kind=kind: (fetch(kind, c).start(), x)[1], 0)
    zeros[...] = jnp.zeros_like(zeros)

    def settle(kind):
        start = pl.multiple_of(last * chunk, chunk)
        tile = tiles[kind, pl.ds(start, chunk)].astype(jnp.float32)
        position = start + lax.broadcasted_iota(jnp.int32, tile.shape, 0)
        fresh = own_ref[pl.ds(group_size, 2)].astype(jnp.float32)[kind : kind + 1]
        tile = jnp.where(position < length, tile, jnp.where(position == length, fresh, 0.0))
        tiles[kind, pl.ds(start, chunk)] = tile.astype(tiles.dtype)

    query = own_ref[...][:group_size]
    scale = 1.0 / math.sqrt(head_dim)

    def score(c, top):
        fetch(0, c).wait()

        @pl.when(c == last)
        def _():
            settle(0)

        start = pl.multiple_of(c * chunk, chunk)
        s = lax.dot_general(
            query, tiles[0, pl.ds(start, chunk)], (((1,), (1,)), ((), ())),
            preferred_element_type=jnp.float32,
        ) * scale
        position = start + lax.broadcasted_iota(jnp.int32, s.shape, 1)
        s = jnp.where(position <= length, s, NEG_FILL)
        scores[:, pl.ds(start, chunk)] = s
        store(0, c).start()
        return jnp.maximum(top, jnp.max(s, axis=1, keepdims=True))

    top = lax.fori_loop(0, live, score, jnp.full((group_size, 1), NEG_FILL, jnp.float32))

    def gather(c, carry):
        total, summed = carry
        fetch(1, c).wait()

        @pl.when(c == last)
        def _():
            settle(1)

        start = pl.multiple_of(c * chunk, chunk)
        s = scores[:, pl.ds(start, chunk)]
        position = start + lax.broadcasted_iota(jnp.int32, s.shape, 1)
        weight = jnp.where(position <= length, jnp.exp(s - top), 0.0)
        high = weight.astype(jnp.bfloat16)
        low = (weight - high.astype(jnp.float32)).astype(jnp.bfloat16)
        both = jnp.concatenate([high, low], axis=0)
        summed = summed + jnp.dot(both, tiles[1, pl.ds(start, chunk)], preferred_element_type=jnp.float32)
        store(1, c).start()
        return total + jnp.sum(weight, axis=1, keepdims=True), summed

    for kind in (0, 1):
        lax.fori_loop(live, chunk_count, lambda c, x, kind=kind: (blank(kind, c).start(), x)[1], 0)

    total, summed = lax.fori_loop(
        0, live, gather,
        (jnp.zeros((group_size, 1), jnp.float32), jnp.zeros((2 * group_size, head_dim), jnp.float32)),
    )
    result = (summed[:group_size] + summed[group_size:]) / total
    for g in range(group_size):
        out_ref[:, g * head_dim : (g + 1) * head_dim] = result[g : g + 1].astype(out_ref.dtype)
    pltpu.make_async_copy(tiles, cache_ref, out_sem).wait()


def attend(perm, lengths, own, gathered, head_count, group_size):
    kinds, total_len, head_dim = gathered.shape
    chunk = min(CHUNK, total_len)
    vmem = pl.BlockSpec(memory_space=pltpu.VMEM)
    smem = pl.BlockSpec(memory_space=pltpu.SMEM)
    any_space = pl.BlockSpec(memory_space=pl.ANY)
    return pl.pallas_call(
        functools.partial(attend_kernel, head_count),
        out_shape=(
            jax.ShapeDtypeStruct(gathered.shape, gathered.dtype),
            jax.ShapeDtypeStruct((1, group_size * head_dim), gathered.dtype),
        ),
        in_specs=[smem, smem, vmem, any_space],
        out_specs=(any_space, vmem),
        scratch_shapes=[
            pltpu.VMEM(gathered.shape, gathered.dtype),
            pltpu.VMEM((chunk, head_dim), gathered.dtype),
            pltpu.VMEM((group_size, total_len), jnp.float32),
            pltpu.SemaphoreType.DMA((kinds, total_len // chunk)),
            pltpu.SemaphoreType.DMA,
        ],
        name="attend",
    )(perm, lengths, own, gathered)


def local(kv_prefill, queries, fresh_kv, lengths, decode_slot_pair):
    devices = lax.axis_size("wide")
    kinds, seq_count, head_count, local_len, head_dim = kv_prefill.shape
    kv_rows = kv_prefill.reshape(kinds, seq_count * head_count, local_len, head_dim)
    fresh = fresh_kv.reshape(kinds, head_dim)
    gathered, own = exchange(decode_slot_pair, queries, fresh, kv_rows, devices)
    cache, attention = attend(
        decode_slot_pair, lengths, own, gathered, head_count, queries.shape[1] // head_dim
    )
    return cache[:, None], attention


def solution(mesh):
    in_specs = (
        P(None, "grp", None, "wide", None),
        P(("grp", "wide"), None),
        P(None, ("grp", "wide"), None),
        P("grp"),
        P("grp"),
    )
    out_specs = (P(None, ("grp", "wide"), None, None), P(("grp", "wide"), None))
    return jax.shard_map(local, mesh=mesh, in_specs=in_specs, out_specs=out_specs, check_vma=False)
```

time: 529 us -> 399 us (0.75)
  blocking collectives: 412 us -> 0 us
  Pallas kernels: 0 us -> 395 us
  local copies, waits for them, and re-layouts: 47.9 us -> 0 us
  starting transfers between devices: 33.7 us -> 0 us
  other arithmetic: 19.9 us -> 0 us
  matrix products: 7.5 us -> 0 us
    all_gather x1 -> x0, blocking collectives: 412 us -> none  [one_gather(): lines, at, finished = (lax.all_gather(flat, axis), 0, [])]
    pallas_call x0 -> x2, Pallas kernels: none -> 395 us  [the longest x1 390 us: exchange(): pl.pallas_call(functools.partial(exchange_kernel, devices), out_shape=(ja...]
    slice x17 -> x0, local copies, waits for them, and re-layouts: 37.5 us -> none  [the longest x15 37.5 us: attend_tile(): decode_cache[1]]
    all_to_all x1 -> x0, starting transfers between devices: 33.7 us -> none  [local(): lax.all_to_all(ordered, 'wide', split_axis=1, concat_axis=2, tiled=True)]
    select_n x6 -> x0, other arithmetic: 15.8 us -> none  [the longest x2 5.3 us: local(): ordered = jnp.take(kv_rows, decode_slot_pair, axis=1)]
    dot_general x30 -> x0, matrix products: 7.5 us -> none  [the longest x15 3.91 us: attend_tile(): jnp.einsum('igd,ibd->igb', own_q, key_tile, preferred_element_type=jnp.fl...]
    gather x2 -> x0, local copies, waits for them, and re-layouts: 5.86 us -> none  [the longest x1 5.2 us: local(): ordered = jnp.take(kv_rows, decode_slot_pair, axis=1)]
  transfers between devices with their start and end apart: 1 -> 0, of which waited for: 0 -> 0; matrix products, arithmetic and copies ran while one was open for 0% -> 0% of each run, Pallas kernels for 0% -> 0%
where the time goes in v1:
time: 399 us; the launch traced here: 396 us
  Pallas kernels  395 us (99%)
    pallas_call x1, Pallas kernels, exchange(): pl.pallas_call(functools.partial(exchange_kernel, devices), out_shape=(ja...  390 us

profile of v1, /device:TPU:45, one launch (start us, length us, event | category | flops | bytes accessed | tf_op | source)
XLA Modules:
  0.0 395.8 jit_solution(7849192010228350450)
XLA Ops:
  0.6 390.5 %exchange.1 = (bf16[2,8192,128]{2,1,0:T(8,128)(2,1)}, bf16[16,128]{1,0:T(8,128)(2,1)}) custom-call(s32[64]{0:T(128)} %perm_ref.3, bf16[1,1024]{1,0:T(2,128)(2,1)} %query_ref.1, bf16[2,128]{1,0:T(2,128)(2,1)} %bitcast.6, bf16[2,64,128,128]{3,2,1,0:T(8,128)(2,1)} %bitcast.5), custom_call_target="tpu_custom_call" | custom-call | tf_op jit(solution)/shard_map/exchange/pallas_call | solution.py:172
  391.1 4.7 %attend.1 = (bf16[2,8192,128]{2,1,0:T(8,128)(2,1)}, bf16[1,1024]{1,0:T(2,128)(2,1)}) custom-call(s32[64]{0:T(128)} %perm_ref.3, s32[8]{0:T(128)} %length_ref.1, bf16[16,128]{1,0:T(8,128)(2,1)} %get-tuple-element.6.own_ref, bf16[2,8192,128]{2,1,0:T(8,128)(2,1)} %get-tuple-element.7.gathered_ref), custom_call_target="tpu_custom_call" | custom-call | tf_op jit(solution)/shard_map/attend/pallas_call | solution.py:295

commit v2 on v1

v2 whole, which is shorter than its diff:
```python
import functools
import math

import jax
import jax.numpy as jnp
from jax import lax
from jax.experimental import pallas as pl
from jax.experimental.pallas import tpu as pltpu
from jax.sharding import PartitionSpec as P

MESH = pl.DeviceIdType.MESH
NEG_FILL = -1e30
PAIR = 2
CHUNK = 1024
EARLY = 8
EXCHANGE_VMEM = 58 << 20
ATTEND_VMEM = 12 << 20


def exchange_kernel(
    devices,
    perm_ref,
    query_ref,
    fresh_ref,
    kv_ref,
    gathered_ref,
    own_ref,
    stage,
    ordered,
    rows,
    passing,
    stage_sem,
    local_sem,
    send_sem,
    recv_sem,
    row_send,
    row_recv,
    near_sem,
    pass_send,
    pass_recv,
):
    chips = devices // 2
    half = chips // 2
    me = lax.axis_index("wide")
    chip = me // 2
    core = lax.rem(me, 2)
    partner = chip * 2 + 1 - core
    local_len = kv_ref.shape[2]

    def device(offset, which):
        return lax.rem(chip + offset + chips, chips) * 2 + which

    def remote(src, dst, send, recv, target):
        return pltpu.make_async_remote_copy(
            src_ref=src,
            dst_ref=dst,
            send_sem=send,
            recv_sem=recv,
            device_id={"wide": target},
            device_id_type=MESH,
        )

    def signal(sem, target):
        pl.semaphore_signal(sem, inc=1, device_id={"wide": target}, device_id_type=MESH)

    barrier = pltpu.get_barrier_semaphore()
    signal(barrier, partner)
    for offset in (1, -1):
        for which in (0, 1):
            signal(barrier, device(offset, which))
    fill = pltpu.make_async_copy(kv_ref, stage, stage_sem)
    fill.start()
    head_dim = kv_ref.shape[3]
    group_size = query_ref.shape[1] // head_dim
    query = query_ref[...].astype(jnp.float32)
    for g in range(0, group_size, PAIR):
        heads = [query[:, h * head_dim : (h + 1) * head_dim] for h in range(g, g + PAIR)]
        rows[0, 0, g // PAIR] = jnp.concatenate(heads, axis=0).astype(jnp.bfloat16)
    rows[0, 0, group_size // PAIR] = fresh_ref[...]
    fill.wait()

    def place(slot):
        ordered[slot] = stage[:, perm_ref[slot]]

    def place_span(first, last):
        def one(k, carry):
            place(lax.rem(chip * 2 + (devices + first) + k, devices))
            return carry

        lax.fori_loop(0, last - first, one, 0)

    place_span(-4, 6)
    pl.semaphore_wait(barrier, 5)

    final = gathered_ref.at[:, pl.ds(me * local_len, local_len)]
    keep = pltpu.make_async_copy(ordered.at[me], final, local_sem)
    keep.start()

    def send_block(target):
        remote(ordered.at[target], final, send_sem, recv_sem, target).start()

    def send_both(distance, cores=(0, 1)):
        for which in cores:
            for sign in (1, -1):
                send_block(device(sign * distance, which))

    def widen(level):
        reach = 1 << level
        for sign in (1, -1):
            signal(near_sem.at[level], device(sign * reach, core))
        pl.semaphore_wait(near_sem.at[level], 2)

    send_block(partner)
    send_both(1, (1,))
    place_span(6, devices - 4)
    sent_to = 1
    level = 0
    while (1 << level) < half:
        widen(level)
        level += 1
        if level < half.bit_length() - 1:
            for distance in range(sent_to + 1, min((1 << level), EARLY) + 1):
                send_both(distance, (distance % 2,))
                sent_to = distance

    turn = 1 - 2 * core

    def row_copy(step):
        size = 1 << step
        return remote(
            rows.at[0, pl.ds(0, size)],
            rows.at[0, pl.ds(size, size)],
            row_send.at[step],
            row_recv.at[step],
            device(turn * (chips >> (step + 1)), core),
        )

    side = jnp.where(chip >= half, 1, -1)

    def turns(c):
        quarter = chips // 4
        return ((c >= chips - quarter) & (lax.rem(c, 2) == 0)) | ((c < quarter) & (lax.rem(c, 2) == 1))

    turned = turns(chip)
    relaying = turns(lax.rem(chip + side + chips, chips))

    def detour():
        both = ordered.at[pl.ds(device(half, 0), 2)]
        return remote(both, passing, pass_send.at[0], pass_recv, device(-side, core))

    def forward(which):
        origin = device(side, core)
        return remote(
            passing.at[which],
            gathered_ref.at[:, pl.ds(origin * local_len, local_len)],
            pass_send.at[1 + which],
            recv_sem,
            device(half + side, which),
        )

    @pl.when(turned)
    def _():
        detour().start()

    @pl.when(jnp.logical_not(turned))
    def _():
        send_block(device(half, 0))
        send_block(device(half, 1))

    row_steps = chips.bit_length() - 1
    row_copy(0).start()
    step = 0
    rounds = [(distance, (0, 1)) for distance in range(half - 1, sent_to, -1)]
    rounds += [(distance, (1 - distance % 2,)) for distance in range(sent_to, 0, -1)]
    for number, (distance, cores) in enumerate(rounds):
        send_both(distance, cores)
        if number == 2:

            @pl.when(relaying)
            def _():
                detour().wait_recv()
                forward(0).start()
                forward(1).start()

        if number % 2 == 1:
            if step < row_steps:
                row_copy(step).wait()
                step += 1
                if step < row_steps:
                    row_copy(step).start()
    while step < row_steps:
        row_copy(step).wait()
        step += 1
        if step < row_steps:
            row_copy(step).start()
    across = remote(rows.at[0], rows.at[1], row_send.at[row_steps], row_recv.at[row_steps], partner)
    across.start()
    across.wait()

    item = perm_ref[me]
    item_core = lax.rem(item, 2)
    same = 1 - lax.rem(item_core + core, 2)
    offset = lax.rem((1 - 2 * item_core) * (chip - item // 2) + chips, chips)
    place_of = 0
    for bit in range(row_steps):
        place_of += lax.rem(offset // (1 << bit), 2) * (chips >> (bit + 1))
    own_ref[...] = rows[1 - same, place_of]

    keep.wait()
    def blocks(count):
        many = ordered.at[pl.ds(0, count)]
        return remote(many, many, send_sem, recv_sem, partner)

    @pl.when(turned)
    def _():
        detour().wait_send()
        blocks(devices - 3).wait_send()

    @pl.when(jnp.logical_not(turned))
    def _():
        blocks(devices - 1).wait_send()

    @pl.when(relaying)
    def _():
        forward(0).wait_send()
        forward(1).wait_send()

    blocks(devices - 1).wait_recv()


def exchange(perm, queries, fresh, kv, devices):
    items, local_len, head_dim = kv.shape[1:]
    chips = devices // 2
    row_steps = chips.bit_length() - 1
    any_space = pl.BlockSpec(memory_space=pl.ANY)
    vmem = pl.BlockSpec(memory_space=pltpu.VMEM)
    row = (queries.shape[1] // head_dim // PAIR + 1, PAIR, head_dim)
    return pl.pallas_call(
        functools.partial(exchange_kernel, devices),
        out_shape=(
            pltpu.VMEM((2, devices * local_len, head_dim), kv.dtype),
            pltpu.VMEM(row, kv.dtype),
        ),
        in_specs=[pl.BlockSpec(memory_space=pltpu.SMEM), vmem, vmem, any_space],
        out_specs=(vmem, vmem),
        scratch_shapes=[
            pltpu.VMEM((2, items, local_len, head_dim), kv.dtype),
            pltpu.VMEM((items, 2, local_len, head_dim), kv.dtype),
            pltpu.VMEM((2, chips, *row), kv.dtype),
            pltpu.VMEM((2, 2, local_len, head_dim), kv.dtype),
            pltpu.SemaphoreType.DMA,
            pltpu.SemaphoreType.DMA,
            pltpu.SemaphoreType.DMA,
            pltpu.SemaphoreType.DMA,
            pltpu.SemaphoreType.DMA((row_steps + 1,)),
            pltpu.SemaphoreType.DMA((row_steps + 1,)),
            pltpu.SemaphoreType.REGULAR((row_steps,)),
            pltpu.SemaphoreType.DMA((3,)),
            pltpu.SemaphoreType.DMA,
        ],
        compiler_params=pltpu.CompilerParams(
            collective_id=0, has_side_effects=True, vmem_limit_bytes=EXCHANGE_VMEM
        ),
        name="exchange",
    )(perm, queries, fresh, kv)


def attend_kernel(
    head_count, perm_ref, length_ref, own_ref, gathered_ref, cache_ref, out_ref,
    edge, zeros, scores, out_sem,
):
    me = lax.axis_index("wide")
    length = length_ref[perm_ref[me] // head_count]
    total_len, head_dim = gathered_ref.shape[1:]
    group_size = scores.shape[0]
    chunk = zeros.shape[0]
    chunk_count = total_len // chunk
    last = length // chunk

    def span(c):
        return pl.ds(pl.multiple_of(c * chunk, chunk), chunk)

    def each(first, stop, source):
        for kind in (0, 1):

            def one(c, carry, kind=kind):
                pltpu.make_async_copy(source(kind, c), cache_ref.at[kind, span(c)], out_sem).start()
                return carry

            lax.fori_loop(first, stop, one, 0)

    each(0, last, lambda kind, c: gathered_ref.at[kind, span(c)])
    zeros[...] = jnp.zeros_like(zeros)
    fresh = own_ref[group_size // PAIR].astype(jnp.float32)
    for kind in (0, 1):
        tile = gathered_ref[kind, span(last)].astype(jnp.float32)
        position = last * chunk + lax.broadcasted_iota(jnp.int32, tile.shape, 0)
        tile = jnp.where(position < length, tile, jnp.where(position == length, fresh[kind : kind + 1], 0.0))
        edge[kind] = tile.astype(edge.dtype)

    query = jnp.concatenate([own_ref[g].astype(jnp.float32) for g in range(group_size // PAIR)], axis=0)
    query = query.astype(own_ref.dtype)
    scale = 1.0 / math.sqrt(head_dim)

    def score(keys):
        s = lax.dot_general(query, keys, (((1,), (1,)), ((), ())), preferred_element_type=jnp.float32)
        return s * scale

    def score_full(c, top):
        s = score(gathered_ref[0, span(c)])
        scores[:, span(c)] = s
        return jnp.maximum(top, jnp.max(s, axis=1, keepdims=True))

    top = lax.fori_loop(0, last, score_full, jnp.full((group_size, 1), NEG_FILL, jnp.float32))
    visible = last * chunk + lax.broadcasted_iota(jnp.int32, (group_size, chunk), 1) <= length
    tail = jnp.where(visible, score(edge[0]), NEG_FILL)
    top = jnp.maximum(top, jnp.max(tail, axis=1, keepdims=True))
    each(last, last + 1, lambda kind, c: edge.at[kind])
    each(last + 1, chunk_count, lambda kind, c: zeros)

    def weigh(weight, values):
        high = weight.astype(jnp.bfloat16)
        low = (weight - high.astype(jnp.float32)).astype(jnp.bfloat16)
        both = jnp.concatenate([high, low], axis=0)
        return jnp.dot(both, values, preferred_element_type=jnp.float32)

    def weigh_full(c, carry):
        total, summed = carry
        weight = jnp.exp(scores[:, span(c)] - top)
        summed = summed + weigh(weight, gathered_ref[1, span(c)])
        return total + jnp.sum(weight, axis=1, keepdims=True), summed

    weight = jnp.where(visible, jnp.exp(tail - top), 0.0)
    total, summed = lax.fori_loop(
        0, last, weigh_full, (jnp.sum(weight, axis=1, keepdims=True), weigh(weight, edge[1]))
    )
    result = (summed[:group_size] + summed[group_size:]) / total
    for g in range(group_size):
        out_ref[:, g * head_dim : (g + 1) * head_dim] = result[g : g + 1].astype(out_ref.dtype)
    pltpu.make_async_copy(gathered_ref, cache_ref, out_sem).wait()


def attend(perm, lengths, own, gathered, head_count, group_size):
    kinds, total_len, head_dim = gathered.shape
    chunk = min(CHUNK, total_len)
    vmem = pl.BlockSpec(memory_space=pltpu.VMEM)
    smem = pl.BlockSpec(memory_space=pltpu.SMEM)
    any_space = pl.BlockSpec(memory_space=pl.ANY)
    return pl.pallas_call(
        functools.partial(attend_kernel, head_count),
        out_shape=(
            jax.ShapeDtypeStruct(gathered.shape, gathered.dtype),
            jax.ShapeDtypeStruct((1, group_size * head_dim), gathered.dtype),
        ),
        in_specs=[smem, smem, vmem, vmem],
        out_specs=(any_space, vmem),
        scratch_shapes=[
            pltpu.VMEM((kinds, chunk, head_dim), gathered.dtype),
            pltpu.VMEM((chunk, head_dim), gathered.dtype),
            pltpu.VMEM((group_size, total_len), jnp.float32),
            pltpu.SemaphoreType.DMA,
        ],
        compiler_params=pltpu.CompilerParams(vmem_limit_bytes=ATTEND_VMEM),
        name="attend",
    )(perm, lengths, own, gathered)


def local(kv_prefill, queries, fresh_kv, lengths, decode_slot_pair):
    devices = lax.axis_size("wide")
    kinds, seq_count, head_count, local_len, head_dim = kv_prefill.shape
    kv_rows = kv_prefill.reshape(kinds, seq_count * head_count, local_len, head_dim)
    fresh = fresh_kv.reshape(kinds, head_dim)
    gathered, own = exchange(decode_slot_pair, queries, fresh, kv_rows, devices)
    cache, attention = attend(
        decode_slot_pair, lengths, own, gathered, head_count, queries.shape[1] // head_dim
    )
    return cache[:, None], attention


def solution(mesh):
    in_specs = (
        P(None, "grp", None, "wide", None),
        P(("grp", "wide"), None),
        P(None, ("grp", "wide"), None),
        P("grp"),
        P("grp"),
    )
    out_specs = (P(None, ("grp", "wide"), None, None), P(("grp", "wide"), None))
    return jax.shard_map(local, mesh=mesh, in_specs=in_specs, out_specs=out_specs, check_vma=False)
```

time: 399 us -> 389 us (0.975)
  Pallas kernels: 395 us -> 384 us
    pallas_call x1, Pallas kernels: 390 us -> 380 us  [exchange(): pl.pallas_call(functools.partial(exchange_kernel, devices), out_shape=(pl...]
where the time goes in v2:
time: 389 us; the launch traced here: 385 us
  Pallas kernels  384 us (99%)
    pallas_call x1, Pallas kernels, exchange(): pl.pallas_call(functools.partial(exchange_kernel, devices), out_shape=(pl...  380 us

profile of v2, /device:TPU:45, one launch (start us, length us, event | category | flops | bytes accessed | tf_op | source)
XLA Modules:
  0.0 384.7 jit_solution(16272958242125214787)
XLA Ops:
  0.6 0.0 copy-start
  0.6 0.0 copy-start.1
  0.7 380.4 %exchange.1 = (bf16[2,8192,128]{2,1,0:T(8,128)(2,1)S(1)}, bf16[5,2,128]{2,1,0:T(2,128)(2,1)S(1)}) custom-call(s32[64]{0:T(128)} %perm_ref.3, bf16[1,1024]{1,0:T(2,128)(2,1)} %query_ref.1, bf16[2,128]{1,0:T(2,128)(2,1)} %bitcast.6, bf16[2,64,128,128]{3,2,1,0:T(8,128)(2,1)} %bitcast.5), custom_call_target="tpu_custom_call" | custom-call | tf_op jit(solution)/shard_map/exchange/pallas_call | solution.py:238
  381.0 0.0 copy-done
  381.1 0.0 copy-done.1
  381.1 3.7 attend.1
Async XLA Ops:
  0.6 380.4 %copy-start = (s32[64]{0:T(128)S(1)}, s32[64]{0:T(128)}, u32[]{:S(2)}) copy-start(s32[64]{0:T(128)} %perm_ref.3) | copy-start | bytes 772
  0.6 380.4 %copy-start.1 = (s32[8]{0:T(128)S(1)}, s32[8]{0:T(128)}, u32[]{:S(2)}) copy-start(s32[8]{0:T(128)} %length_ref.1) | copy-start | bytes 100

commit v3 on v2

--- a/solution.py
+++ b/solution.py
@@ -11,15 +11,16 @@
 MESH = pl.DeviceIdType.MESH
 NEG_FILL = -1e30
 PAIR = 2
-CHUNK = 1024
-EARLY = 8
+CHUNK = 512
+WIDE = 2048
+EARLY = 5
 EXCHANGE_VMEM = 58 << 20
 ATTEND_VMEM = 12 << 20
 
 
 def exchange_kernel(
     devices,
-    perm_ref,
+    perm_source,
     query_ref,
     fresh_ref,
     kv_ref,
@@ -38,6 +39,10 @@
     near_sem,
     pass_send,
     pass_recv,
+    query_row,
+    fresh_rows,
+    small_sem,
+    perm_ref,
 ):
     chips = devices // 2
     half = chips // 2
@@ -69,14 +74,16 @@
         for which in (0, 1):
             signal(barrier, device(offset, which))
     fill = pltpu.make_async_copy(kv_ref, stage, stage_sem)
+    slots_in = pltpu.make_async_copy(perm_source, perm_ref, small_sem.at[2])
+    slots_in.start()
     fill.start()
-    head_dim = kv_ref.shape[3]
-    group_size = query_ref.shape[1] // head_dim
-    query = query_ref[...].astype(jnp.float32)
-    for g in range(0, group_size, PAIR):
-        heads = [query[:, h * head_dim : (h + 1) * head_dim] for h in range(g, g + PAIR)]
-        rows[0, 0, g // PAIR] = jnp.concatenate(heads, axis=0).astype(jnp.bfloat16)
-    rows[0, 0, group_size // PAIR] = fresh_ref[...]
+    bring = [
+        pltpu.make_async_copy(query_ref, query_row, small_sem.at[0]),
+        pltpu.make_async_copy(fresh_ref, fresh_rows, small_sem.at[1]),
+    ]
+    for copy in bring:
+        copy.start()
+    slots_in.wait()
     fill.wait()
 
     def place(slot):
@@ -113,6 +120,15 @@
     send_block(partner)
     send_both(1, (1,))
     place_span(6, devices - 4)
+    for copy in bring:
+        copy.wait()
+    head_dim = kv_ref.shape[3]
+    group_size = query_ref.shape[1] // head_dim
+    query = query_row[...].astype(jnp.float32)
+    for g in range(0, group_size, PAIR):
+        heads = [query[:, h * head_dim : (h + 1) * head_dim] for h in range(g, g + PAIR)]
+        rows[0, 0, g // PAIR] = jnp.concatenate(heads, axis=0).astype(jnp.bfloat16)
+    rows[0, 0, group_size // PAIR] = fresh_rows[...]
     sent_to = 1
     level = 0
     while (1 << level) < half:
@@ -241,7 +257,7 @@
             pltpu.VMEM((2, devices * local_len, head_dim), kv.dtype),
             pltpu.VMEM(row, kv.dtype),
         ),
-        in_specs=[pl.BlockSpec(memory_space=pltpu.SMEM), vmem, vmem, any_space],
+        in_specs=[any_space] * 4,
         out_specs=(vmem, vmem),
         scratch_shapes=[
             pltpu.VMEM((2, items, local_len, head_dim), kv.dtype),
@@ -257,6 +273,10 @@
             pltpu.SemaphoreType.REGULAR((row_steps,)),
             pltpu.SemaphoreType.DMA((3,)),
             pltpu.SemaphoreType.DMA,
+            pltpu.VMEM(queries.shape, kv.dtype),
+            pltpu.VMEM(fresh.shape, kv.dtype),
+            pltpu.SemaphoreType.DMA((3,)),
+            pltpu.SMEM(perm.shape, perm.dtype),
         ],
         compiler_params=pltpu.CompilerParams(
             collective_id=0, has_side_effects=True, vmem_limit_bytes=EXCHANGE_VMEM
@@ -298,43 +318,43 @@
         tile = jnp.where(position < length, tile, jnp.where(position == length, fresh[kind : kind + 1], 0.0))
         edge[kind] = tile.astype(edge.dtype)
 
-    query = jnp.concatenate([own_ref[g].astype(jnp.float32) for g in range(group_size // PAIR)], axis=0)
-    query = query.astype(own_ref.dtype)
+    heads = jnp.concatenate([own_ref[g].astype(jnp.float32) for g in range(group_size // PAIR)], axis=0)
+    query = heads.astype(own_ref.dtype)
     scale = 1.0 / math.sqrt(head_dim)
-
-    def score(keys):
+    wide = min(WIDE, total_len)
+    turns = (length + wide - 1) // wide
+    newest = jnp.sum(heads * fresh[0:1], axis=1, keepdims=True) * scale
+
+    def wide_span(c):
+        return pl.ds(pl.multiple_of(c * wide, wide), wide)
+
+    def score(c, top):
+        keys = gathered_ref[0, wide_span(c)]
         s = lax.dot_general(query, keys, (((1,), (1,)), ((), ())), preferred_element_type=jnp.float32)
-        return s * scale
-
-    def score_full(c, top):
-        s = score(gathered_ref[0, span(c)])
-        scores[:, span(c)] = s
+        position = c * wide + lax.broadcasted_iota(jnp.int32, s.shape, 1)
+        s = jnp.where(position < length, s * scale, NEG_FILL)
+        scores[:, wide_span(c)] = s
         return jnp.maximum(top, jnp.max(s, axis=1, keepdims=True))
 
-    top = lax.fori_loop(0, last, score_full, jnp.full((group_size, 1), NEG_FILL, jnp.float32))
-    visible = last * chunk + lax.broadcasted_iota(jnp.int32, (group_size, chunk), 1) <= length
-    tail = jnp.where(visible, score(edge[0]), NEG_FILL)
-    top = jnp.maximum(top, jnp.max(tail, axis=1, keepdims=True))
+    top = lax.fori_loop(0, turns, score, newest)
     each(last, last + 1, lambda kind, c: edge.at[kind])
     each(last + 1, chunk_count, lambda kind, c: zeros)
 
-    def weigh(weight, values):
+    def weigh(c, carry):
+        total, summed = carry
+        weight = jnp.exp(scores[:, wide_span(c)] - top)
         high = weight.astype(jnp.bfloat16)
         low = (weight - high.astype(jnp.float32)).astype(jnp.bfloat16)
         both = jnp.concatenate([high, low], axis=0)
-        return jnp.dot(both, values, preferred_element_type=jnp.float32)
-
-    def weigh_full(c, carry):
-        total, summed = carry
-        weight = jnp.exp(scores[:, span(c)] - top)
-        summed = summed + weigh(weight, gathered_ref[1, span(c)])
+        values = gathered_ref[1, wide_span(c)]
+        summed = summed + jnp.dot(both, values, preferred_element_type=jnp.float32)
         return total + jnp.sum(weight, axis=1, keepdims=True), summed
 
-    weight = jnp.where(visible, jnp.exp(tail - top), 0.0)
+    weight = jnp.exp(newest - top)
     total, summed = lax.fori_loop(
-        0, last, weigh_full, (jnp.sum(weight, axis=1, keepdims=True), weigh(weight, edge[1]))
+        0, turns, weigh, (weight, jnp.zeros((2 * group_size, head_dim), jnp.float32))
     )
-    result = (summed[:group_size] + summed[group_size:]) / total
+    result = (summed[:group_size] + summed[group_size:] + weight * fresh[1:2]) / total
     for g in range(group_size):
         out_ref[:, g * head_dim : (g + 1) * head_dim] = result[g : g + 1].astype(out_ref.dtype)
     pltpu.make_async_copy(gathered_ref, cache_ref, out_sem).wait()

time: 389 us -> 387 us (level)
  no operation moved by 1% of the time
where the time goes in v3:
time: 387 us; the launch traced here: 385 us
  Pallas kernels  384 us (99%)
    pallas_call x1, Pallas kernels, exchange(): pl.pallas_call(functools.partial(exchange_kernel, devices), out_shape=(pl...  380 us

profile of v3, /device:TPU:45, one launch (start us, length us, event | category | flops | bytes accessed | tf_op | source)
XLA Modules:
  0.0 384.8 jit_solution(14575500580833327513)
XLA Ops:
  0.6 0.0 copy-start
  0.6 0.0 copy-start.1
  0.7 380.5 %exchange.1 = (bf16[2,8192,128]{2,1,0:T(8,128)(2,1)S(1)}, bf16[5,2,128]{2,1,0:T(2,128)(2,1)S(1)}) custom-call(s32[64]{0:T(128)} %perm_ref.1, bf16[1,1024]{1,0:T(2,128)(2,1)} %query_ref.1, bf16[2,128]{1,0:T(2,128)(2,1)} %bitcast.6, bf16[2,64,128,128]{3,2,1,0:T(8,128)(2,1)} %bitcast.5), custom_call_target="tpu_custom_call" | custom-call | tf_op jit(solution)/shard_map/exchange/pallas_call | solution.py:254
  381.1 0.0 copy-done
  381.2 0.0 copy-done.1
  381.2 3.6 attend.1
Async XLA Ops:
  0.6 380.5 %copy-start = (s32[64]{0:T(128)S(1)}, s32[64]{0:T(128)}, u32[]{:S(2)}) copy-start(s32[64]{0:T(128)} %perm_ref.1) | copy-start | bytes 772
  0.6 380.5 %copy-start.1 = (s32[8]{0:T(128)S(1)}, s32[8]{0:T(128)}, u32[]{:S(2)}) copy-start(s32[8]{0:T(128)} %length_ref.1) | copy-start | bytes 100

commit v4 on v3

--- a/solution.py
+++ b/solution.py
@@ -287,7 +287,7 @@
 
 def attend_kernel(
     head_count, perm_ref, length_ref, own_ref, gathered_ref, cache_ref, out_ref,
-    edge, zeros, scores, out_sem,
+    edge, zeros, scores, out_row, out_sem, row_sem,
 ):
     me = lax.axis_index("wide")
     length = length_ref[perm_ref[me] // head_count]
@@ -356,8 +356,11 @@
     )
     result = (summed[:group_size] + summed[group_size:] + weight * fresh[1:2]) / total
     for g in range(group_size):
-        out_ref[:, g * head_dim : (g + 1) * head_dim] = result[g : g + 1].astype(out_ref.dtype)
+        out_row[:, g * head_dim : (g + 1) * head_dim] = result[g : g + 1].astype(out_row.dtype)
+    deliver = pltpu.make_async_copy(out_row, out_ref, row_sem)
+    deliver.start()
     pltpu.make_async_copy(gathered_ref, cache_ref, out_sem).wait()
+    deliver.wait()
 
 
 def attend(perm, lengths, own, gathered, head_count, group_size):
@@ -373,11 +376,13 @@
             jax.ShapeDtypeStruct((1, group_size * head_dim), gathered.dtype),
         ),
         in_specs=[smem, smem, vmem, vmem],
-        out_specs=(any_space, vmem),
+        out_specs=(any_space, any_space),
         scratch_shapes=[
             pltpu.VMEM((kinds, chunk, head_dim), gathered.dtype),
             pltpu.VMEM((chunk, head_dim), gathered.dtype),
             pltpu.VMEM((group_size, total_len), jnp.float32),
+            pltpu.VMEM((1, group_size * head_dim), gathered.dtype),
+            pltpu.SemaphoreType.DMA,
             pltpu.SemaphoreType.DMA,
         ],
         compiler_params=pltpu.CompilerParams(vmem_limit_bytes=ATTEND_VMEM),

time: 387 us -> 387 us (level)
  no operation moved by 1% of the time
where the time goes in v4:
time: 387 us; the launch traced here: 384 us
  Pallas kernels  384 us (99%)
    pallas_call x1, Pallas kernels, exchange(): pl.pallas_call(functools.partial(exchange_kernel, devices), out_shape=(pl...  380 us

profile of v4, /device:TPU:45, one launch (start us, length us, event | category | flops | bytes accessed | tf_op | source)
XLA Modules:
  0.0 384.3 jit_solution(5910609576867789462)
XLA Ops:
  0.6 0.0 copy-start
  0.6 0.0 copy-start.1
  0.7 380.5 %exchange.1 = (bf16[2,8192,128]{2,1,0:T(8,128)(2,1)S(1)}, bf16[5,2,128]{2,1,0:T(2,128)(2,1)S(1)}) custom-call(s32[64]{0:T(128)} %perm_ref.1, bf16[1,1024]{1,0:T(2,128)(2,1)} %query_ref.1, bf16[2,128]{1,0:T(2,128)(2,1)} %bitcast.6, bf16[2,64,128,128]{3,2,1,0:T(8,128)(2,1)} %bitcast.5), custom_call_target="tpu_custom_call" | custom-call | tf_op jit(solution)/shard_map/exchange/pallas_call | solution.py:254
  381.1 0.0 copy-done
  381.2 0.0 copy-done.1
  381.2 3.1 attend.1
Async XLA Ops:
  0.6 380.5 %copy-start = (s32[64]{0:T(128)S(1)}, s32[64]{0:T(128)}, u32[]{:S(2)}) copy-start(s32[64]{0:T(128)} %perm_ref.1) | copy-start | bytes 772
  0.6 380.5 %copy-start.1 = (s32[8]{0:T(128)S(1)}, s32[8]{0:T(128)}, u32[]{:S(2)}) copy-start(s32[8]{0:T(128)} %length_ref.1) | copy-start | bytes 100
